TPU v7x, 32 devices: a whole 2x2x4 slice. The times are simulated.
32 devices in a mesh: pb: 4 (over z), ka: 8 (over y, x, core).
Axes of the slice: x: 2, y: 2, z: 4, core: 2. Of those that a mesh axis runs over, the one named last changes fastest.
Arguments:
- queries: float32 [1, 4096, 128], P(None, ('pb', 'ka')), may hold values from -6 to 6
- keys: float32 [1, 4096, 128], P(None, ('ka', 'pb')), may hold values from -6 to 6
- values: float32 [1, 4096, 128], P(None, ('ka', 'pb')), may hold values from -6 to 6
- tangent_q: float32 [1, 4096, 128], P(None, ('pb', 'ka')), may hold values from -6 to 6
- tangent_k: float32 [1, 4096, 128], P(None, ('ka', 'pb')), may hold values from -6 to 6
- tangent_v: float32 [1, 4096, 128], P(None, ('ka', 'pb')), may hold values from -6 to 6
Outputs:
- attended: float32 [1, 4096, 128], P(None, ('pb', 'ka'))
- attended_tangent: float32 [1, 4096, 128], P(None, ('pb', 'ka'))
All inputs are finite; a program needn't handle non-finite values.
Results may differ from a plain program's by a relative error of at most 0.0003.
Values sent between devices are 32-bit elements; how exact they have to be, the bound alone decides.
No kernel may reach another device: no remote copies, remote signals or barrier semaphores. Data moves between devices by JAX's collectives and lax.ppermute only.
A program may use at most 128 MiB of HBM per device.

v0:
```python
import jax
import jax.numpy as jnp
from jax import lax
from jax.sharding import PartitionSpec as P


def combined_all(value, axis, join):
    pieces = jax.tree.map(lambda part: lax.all_gather(part, axis), value)
    head = jax.tree.map(lambda part: part[0], pieces)
    tail = jax.tree.map(lambda part: part[1:], pieces)
    so_far, _ = lax.scan(lambda so_far, share: (join(so_far, share), None), head, tail)
    return so_far


def join_partials(first, second):
    peak = jnp.maximum(first[0], second[0])
    left = jnp.exp(first[0] - peak)
    right = jnp.exp(second[0] - peak)
    total = first[1] * left + second[1] * right
    numer = first[2] * left[..., None] + second[2] * right[..., None]
    tnumer = first[3] * left[..., None] + second[3] * right[..., None]
    drift = first[4] * left + second[4] * right
    return (peak, total, numer, tnumer, drift)


def body(queries, keys, values, tangent_q, tangent_k, tangent_v):
    highest = lax.Precision.HIGHEST
    head_count, _, width = queries.shape
    factor = width ** (-0.5)
    all_q, all_dq = (
        lax.all_gather(queries, "ka", axis=1, tiled=True),
        lax.all_gather(tangent_q, "ka", axis=1, tiled=True),
    )
    span = all_q.shape[1]
    block = min(512, span)
    blocks = span // block
    split_q = all_q.reshape(head_count, blocks, block, width)
    split_dq = all_dq.reshape(head_count, blocks, block, width)
    start_state = (
        jnp.full((head_count, span), -1e30, jnp.float32),
        jnp.zeros((head_count, span), jnp.float32),
        jnp.zeros((head_count, span, width), jnp.float32),
        jnp.zeros((head_count, span, width), jnp.float32),
        jnp.zeros((head_count, span), jnp.float32),
    )
    piece_k = lax.all_gather(keys, "pb", axis=1, tiled=True)
    piece_dk = lax.all_gather(tangent_k, "pb", axis=1, tiled=True)
    piece_v = lax.all_gather(values, "pb", axis=1, tiled=True)
    piece_dv = lax.all_gather(tangent_v, "pb", axis=1, tiled=True)
    shaped = (
        start_state[0].reshape(head_count, blocks, block),
        start_state[1].reshape(head_count, blocks, block),
        start_state[2].reshape(head_count, blocks, block, width),
        start_state[3].reshape(head_count, blocks, block, width),
        start_state[4].reshape(head_count, blocks, block),
    )

    def one_head(items):
        (
            head_q,
            head_dq,
            head_k,
            head_dk,
            head_v,
            head_dv,
            peak_h,
            total_h,
            numer_h,
            tnumer_h,
            drift_h,
        ) = items

        def one_block(parts):
            query_blk, dquery_blk, old_peak, old_total, old_numer, old_tnumer, old_drift = parts
            scores = jnp.dot(query_blk, head_k.T, precision=highest) * factor
            tangent = (
                jnp.dot(dquery_blk, head_k.T, precision=highest)
                + jnp.dot(query_blk, head_dk.T, precision=highest)
            ) * factor
            new_peak = jnp.maximum(old_peak, jnp.max(scores, axis=1))
            rescale = jnp.exp(old_peak - new_peak)
            weights = jnp.exp(scores - new_peak[:, None])
            product = weights * tangent
            new_total = old_total * rescale + jnp.sum(weights, axis=1)
            new_numer = old_numer * rescale[:, None] + jnp.dot(weights, head_v, precision=highest)
            new_tnumer = (
                old_tnumer * rescale[:, None]
                + jnp.dot(weights, head_dv, precision=highest)
                + jnp.dot(product, head_v, precision=highest)
            )
            new_drift = old_drift * rescale + jnp.sum(product, axis=1)
            return (new_peak, new_total, new_numer, new_tnumer, new_drift)

        return lax.map(one_block, (head_q, head_dq, peak_h, total_h, numer_h, tnumer_h, drift_h))

    result = lax.map(one_head, (split_q, split_dq, piece_k, piece_dk, piece_v, piece_dv) + shaped)
    peak = result[0].reshape(head_count, span)
    total = result[1].reshape(head_count, span)
    numer = result[2].reshape(head_count, span, width)
    tnumer = result[3].reshape(head_count, span, width)
    drift = result[4].reshape(head_count, span)
    merged = combined_all((peak, total, numer, tnumer, drift), "ka", join_partials)
    owned = span // lax.axis_size("ka")
    offset = lax.axis_index("ka") * owned
    total = lax.dynamic_slice_in_dim(merged[1], offset, owned, 1)
    numer = lax.dynamic_slice_in_dim(merged[2], offset, owned, 1)
    tnumer = lax.dynamic_slice_in_dim(merged[3], offset, owned, 1)
    drift = lax.dynamic_slice_in_dim(merged[4], offset, owned, 1)
    attended = numer / total[..., None]
    attended_tangent = tnumer / total[..., None] - attended * (drift / total)[..., None]
    return (attended, attended_tangent)


def solution(mesh):
    return jax.shard_map(
        body,
        mesh=mesh,
        in_specs=(
            P(None, ("pb", "ka"), None),
            P(None, ("ka", "pb"), None),
            P(None, ("ka", "pb"), None),
            P(None, ("pb", "ka"), None),
            P(None, ("ka", "pb"), None),
            P(None, ("ka", "pb"), None),
        ),
        out_specs=(P(None, ("pb", "ka"), None), P(None, ("pb", "ka"), None)),
        check_vma=False,
    )
```

profile of v0, /device:TPU:0, one launch (start us, length us, event | category | flops | bytes accessed | tf_op | source)
XLA Modules:
  0.0 214.0 jit_solution(3527905628978141757)
XLA Ops:
  7.3 15.9 %all_gather.34 = f32[1,512,128]{2,1,0:T(8,128)S(1)} all-gather(f32[1,128,128]{2,1,0:T(8,128)} %param.11), channel_id=1, replica_groups=mesh['pb'=4,'ka'=8] {'pb'}, dimensions={1}, use_global_device_ids=true | all-gather | bytes 327680 | tf_op jit(solution)/shard_map/all_gather | solution.py:46
  23.1 14.9 %all_gather.35 = f32[1,512,128]{2,1,0:T(8,128)S(1)} all-gather(f32[1,128,128]{2,1,0:T(8,128)} %param.12), channel_id=1, replica_groups=mesh['pb'=4,'ka'=8] {'pb'}, dimensions={1}, use_global_device_ids=true | all-gather | bytes 327680 | tf_op jit(solution)/shard_map/all_gather | solution.py:48
  38.0 14.0 %all_gather.38 = f32[1,512,128]{2,1,0:T(8,128)S(1)} all-gather(f32[1,128,128]{2,1,0:T(8,128)} %param.14), channel_id=1, replica_groups=mesh['pb'=4,'ka'=8] {'pb'}, dimensions={1}, use_global_device_ids=true | all-gather | bytes 327680 | tf_op jit(solution)/shard_map/all_gather | solution.py:47
  52.1 16.6 %all_gather.36 = f32[1,512,128]{2,1,0:T(8,128)} all-gather(f32[1,128,128]{2,1,0:T(8,128)} %param.15), channel_id=1, replica_groups=mesh['pb'=4,'ka'=8] {'pb'}, dimensions={1}, use_global_device_ids=true | all-gather | bytes 327680 | tf_op jit(solution)/shard_map/all_gather | solution.py:49
  68.6 10.1 %all_gather.33 = f32[1,1024,128]{2,1,0:T(8,128)S(1)} all-gather(f32[1,128,128]{2,1,0:T(8,128)} %param.10), channel_id=1, replica_groups=mesh['pb'=4,'ka'=8] {'ka'}, dimensions={1}, use_global_device_ids=true | all-gather | bytes 589824 | tf_op jit(solution)/shard_map/all_gather | solution.py:31
  78.8 10.8 %all_gather.37 = f32[1,1024,128]{2,1,0:T(8,128)} all-gather(f32[1,128,128]{2,1,0:T(8,128)} %param.13), channel_id=1, replica_groups=mesh['pb'=4,'ka'=8] {'ka'}, dimensions={1}, use_global_device_ids=true | all-gather | bytes 589824 | tf_op jit(solution)/shard_map/all_gather | solution.py:32
  89.5 24.6 %while.53 = (s32[]{:T(128)}, f32[2,512]{1,0:T(2,128)S(1)}, f32[2,512]{1,0:T(2,128)S(1)}, f32[2,512,128]{2,1,0:T(8,128)}, f32[2,512,128]{2,1,0:T(8,128)}, /*index...) while((s32[]{:T(128)}, f32[2,512]{1,0:T(2,128)S(1)}, ...), condition=%wide.region_4.5_spmd, body=%wide.region_0.4_spmd.sunk | while | flops 2419001344 | bytes 12892333 | solution.py:94
  89.5 1.9 fusion.66
  94.0 2.8 %convolution_add_fusion.5 = f32[512,128]{1,0:T(8,128)S(1)} fusion(f32[512,128]{1,0:T(8,128)} %get-tuple-element.549, f32[512,512]{0,1:T(8,128)S(1)} %get-tuple-element.489, f32[512]{0:T(512)S(1)} %get-tuple-element.488, f32[512]{0:T(512)S(1)} %get-tuple-element.492), kind=kOutput, calls=%fused_computation.7.clone.1 | convolution fusion | flops 402980864 | bytes 1576960 | tf_op jit(solution)/shard_map/while/body/eval_jaxpr/while/body/eval_jaxpr/dot_general | solution.py:88
  96.8 2.5 %fusion.71 = f32[2,512,128]{2,1,0:T(8,128)} fusion(f32[2,512,128]{2,1,0:T(8,128)} %get-tuple-element.530, s32[]{:T(128)S(6)} %copy.19, f32[512,128]{1,0:T(8,128)S(1)} %convolution_add_fusion.5, f32[512,512]{0,1:T(8,128)S(1)} %get-tuple-element.493, f32[512,128]{1,0:T(8,128)S(1)} %get-tuple-element.548), kind=kOutput, calls=%fused_computation.6.clone.1 | convolution fusion | flops 402718720 | bytes 1835012 | tf_op jit(solution)/shard_map/while/body/eval_jaxpr/while/body/eval_jaxpr/dot_general | solution.py:89
  99.3 2.5 %fusion.70 = f32[2,512,128]{2,1,0:T(8,128)} fusion(f32[2,512,128]{2,1,0:T(8,128)} %get-tuple-element.529, s32[]{:T(128)S(6)} %copy.19, f32[512,128]{1,0:T(8,128)S(1)} %get-tuple-element.548, f32[512,512]{0,1:T(8,128)S(1)} %get-tuple-element.489, f32[512]{0:T(512)S(1)} %get-tuple-element.488, f32[512]{0:T(512)S(1)} %get-tuple-element.492), kind=kOutput, calls=%fused_computation.10.clone.1 | convolution fusion | flops 402980864 | bytes 1576964 | tf_op jit(solution)/shard_map/while/body/eval_jaxpr/while/body/eval_jaxpr/dot_general | solution.py:85
  101.9 1.9 fusion.66
  106.4 2.8 %convolution_add_fusion.5 = f32[512,128]{1,0:T(8,128)S(1)} fusion(f32[512,128]{1,0:T(8,128)} %get-tuple-element.549, f32[512,512]{0,1:T(8,128)S(1)} %get-tuple-element.489, f32[512]{0:T(512)S(1)} %get-tuple-element.488, f32[512]{0:T(512)S(1)} %get-tuple-element.492), kind=kOutput, calls=%fused_computation.7.clone.1 | convolution fusion | flops 402980864 | bytes 1576960 | tf_op jit(solution)/shard_map/while/body/eval_jaxpr/while/body/eval_jaxpr/dot_general | solution.py:88
  109.1 2.5 %fusion.71 = f32[2,512,128]{2,1,0:T(8,128)} fusion(f32[2,512,128]{2,1,0:T(8,128)} %get-tuple-element.530, s32[]{:T(128)S(6)} %copy.19, f32[512,128]{1,0:T(8,128)S(1)} %convolution_add_fusion.5, f32[512,512]{0,1:T(8,128)S(1)} %get-tuple-element.493, f32[512,128]{1,0:T(8,128)S(1)} %get-tuple-element.548), kind=kOutput, calls=%fused_computation.6.clone.1 | convolution fusion | flops 402718720 | bytes 1835012 | tf_op jit(solution)/shard_map/while/body/eval_jaxpr/while/body/eval_jaxpr/dot_general | solution.py:89
  111.7 2.5 %fusion.70 = f32[2,512,128]{2,1,0:T(8,128)} fusion(f32[2,512,128]{2,1,0:T(8,128)} %get-tuple-element.529, s32[]{:T(128)S(6)} %copy.19, f32[512,128]{1,0:T(8,128)S(1)} %get-tuple-element.548, f32[512,512]{0,1:T(8,128)S(1)} %get-tuple-element.489, f32[512]{0:T(512)S(1)} %get-tuple-element.488, f32[512]{0:T(512)S(1)} %get-tuple-element.492), kind=kOutput, calls=%fused_computation.10.clone.1 | convolution fusion | flops 402980864 | bytes 1576964 | tf_op jit(solution)/shard_map/while/body/eval_jaxpr/while/body/eval_jaxpr/dot_general | solution.py:85
  115.0 8.8 %all_gather.40 = f32[8,1,1024]{2,1,0:T(1,128)S(1)} all-gather(f32[1,1,1024]{2,1,0:T(1,128)S(1)} %all_gather_reshape.16), channel_id=1, replica_groups=mesh['pb'=4,'ka'=8] {'ka'}, dimensions={0}, use_global_device_ids=true | all-gather | bytes 36864 | tf_op jit(solution)/shard_map/all_gather | solution.py:8
  123.8 8.6 %all_gather.39 = f32[8,1,1024]{2,1,0:T(1,128)S(1)} all-gather(f32[1,1,1024]{2,1,0:T(1,128)S(1)} %all_gather_reshape.15), channel_id=1, replica_groups=mesh['pb'=4,'ka'=8] {'ka'}, dimensions={0}, use_global_device_ids=true | all-gather | bytes 36864 | tf_op jit(solution)/shard_map/all_gather | solution.py:8
  132.4 9.0 %all_gather.43 = f32[8,1,1024]{2,1,0:T(1,128)S(1)} all-gather(f32[1,1,1024]{2,1,0:T(1,128)S(1)} %all_gather_reshape.19), channel_id=1, replica_groups=mesh['pb'=4,'ka'=8] {'ka'}, dimensions={0}, use_global_device_ids=true | all-gather | bytes 36864 | tf_op jit(solution)/shard_map/all_gather | solution.py:8
  141.4 8.8 %all-gather.5.cloned.1.call-done = f32[8,1,1024,128]{3,2,1,0:T(8,128)} async-done(((f32[1,1,1024,128]{3,2,1,0:T(8,128)}), f32[8,1,1024,128]{3,2,1,0:T(8,128)}) %all-gather.5.cloned.1.call-update) | async-done | bytes 4194320 | tf_op jit(solution)/shard_map/all_gather | solution.py:8
  150.2 4.1 %slice.48 = f32[7,1,1024,128]{3,2,1,0:T(8,128)} slice(f32[8,1,1024,128]{3,2,1,0:T(8,128)} %all-gather.5.cloned.1.call-done), slice={[1:8], [0:1], [0:1024], [0:128]} | slice | bytes 7340032 | tf_op jit(solution)/shard_map/slice | solution.py:10
  155.4 33.3 %all-gather.3.cloned.1.call-done = f32[8,1,1024,128]{3,2,1,0:T(8,128)} async-done(((f32[1,1,1024,128]{3,2,1,0:T(8,128)}), f32[8,1,1024,128]{3,2,1,0:T(8,128)}) %all-gather.3.cloned.1.call-update) | async-done | bytes 4194320 | tf_op jit(solution)/shard_map/all_gather | solution.py:8
  189.8 4.1 %slice.47 = f32[7,1,1024,128]{3,2,1,0:T(8,128)} slice(f32[8,1,1024,128]{3,2,1,0:T(8,128)} %all-gather.3.cloned.1.call-done), slice={[1:8], [0:1], [0:1024], [0:128]} | slice | bytes 7340032 | tf_op jit(solution)/shard_map/slice | solution.py:10
  193.8 12.5 %while.54 = (s32[]{:T(128)}, f32[1,1024]{1,0:T(1,128)S(1)}, f32[1,1024]{1,0:T(1,128)S(1)}, f32[1,1024,128]{2,1,0:T(8,128)S(1)}, f32[1,1024,128]{2,1,0:T(8,128)S(...) while((s32[]{:T(128)}, f32[1,1024]{1,0:T(1,128)S(1)}, ...), condition=%wide.region_6.7_spmd, body=%wide.region_5.6_spmd.sunk | while | flops 795650 | bytes 3207305 | solution.py:11
  193.9 1.7 fusion.74
  (67 shorter events, 19.5 us)
Async XLA Ops:
  7.2 143.0 %all-gather.5.cloned.1.call-start = ((), (), s32[]{:S(2)}) async-start(), calls=%async_computation.1 | async-start | bytes 4718592 | tf_op jit(solution)/shard_map/all_gather | solution.py:8
  114.2 74.5 %all-gather.3.cloned.1.call-start = ((), (), s32[]{:S(2)}) async-start(), calls=%async_computation | async-start | bytes 4718592 | tf_op jit(solution)/shard_map/all_gather | solution.py:8
  123.8 31.5 %copy-start = (f32[8,1,1024]{2,1,0:T(1,128)}, f32[8,1,1024]{2,1,0:T(1,128)S(1)}, u32[]{:S(2)}) copy-start(f32[8,1,1024]{2,1,0:T(1,128)S(1)} %all_gather.40) | copy-start | bytes 98308
  132.4 22.9 %copy-start.1 = (f32[8,1,1024]{2,1,0:T(1,128)}, f32[8,1,1024]{2,1,0:T(1,128)S(1)}, u32[]{:S(2)}) copy-start(f32[8,1,1024]{2,1,0:T(1,128)S(1)} %all_gather.39) | copy-start | bytes 98308
  141.4 13.9 %copy-start.2 = (f32[8,1,1024]{2,1,0:T(1,128)}, f32[8,1,1024]{2,1,0:T(1,128)S(1)}, u32[]{:S(2)}) copy-start(f32[8,1,1024]{2,1,0:T(1,128)S(1)} %all_gather.43) | copy-start | bytes 98308
  188.7 5.2 %slice-start = ((f32[8,1,1024]{2,1,0:T(1,128)}), f32[7,1,1024]{2,1,0:T(1,128)S(1)}, s32[]{:S(2)}) async-start(f32[8,1,1024]{2,1,0:T(1,128)} %copy-done), calls=%async_computation.2 | async-start | bytes 57344 | tf_op jit(solution)/shard_map/slice | solution.py:10
  188.7 5.2 %slice-start.1 = ((f32[8,1,1024]{2,1,0:T(1,128)}), f32[7,1,1024]{2,1,0:T(1,128)S(1)}, s32[]{:S(2)}) async-start(f32[8,1,1024]{2,1,0:T(1,128)} %copy-done.1), calls=%async_computation.3 | async-start | bytes 57344 | tf_op jit(solution)/shard_map/slice | solution.py:10
  188.7 5.2 %slice-start.2 = ((f32[8,1,1024]{2,1,0:T(1,128)}), f32[7,1,1024]{2,1,0:T(1,128)S(1)}, s32[]{:S(2)}) async-start(f32[8,1,1024]{2,1,0:T(1,128)} %copy-done.2), calls=%async_computation.4 | async-start | bytes 57344 | tf_op jit(solution)/shard_map/slice | solution.py:10
Sparse Core Ops, SparseCore 0:
  114.3 35.8 all-gather.4
  152.1 36.5 all-gather.2
where the time goes:
time: 215 us; the launch traced here: 214 us
  blocking collectives  109 us (51%)
  waiting for transfers between devices  42.8 us (20%)
  matrix products  23.9 us (11%)
  between operations  14.1 us (7%)
  other arithmetic  13.6 us (6%)
  local copies, waits for them, and re-layouts  10.6 us (5%)
    all_gather x2, waiting for transfers between devices, combined_all(): pieces = jax.tree.map(lambda part: lax.all_gather(part, axis), value)  42.1 us
    all_gather x3, blocking collectives, combined_all(): pieces = jax.tree.map(lambda part: lax.all_gather(part, axis), value)  26.4 us
    all_gather x1, blocking collectives, body(): piece_dv = lax.all_gather(tangent_v, 'pb', axis=1, tiled=True)  16.6 us
    all_gather x1, blocking collectives, body(): piece_k = lax.all_gather(keys, 'pb', axis=1, tiled=True)  15.9 us
    all_gather x1, blocking collectives, body(): piece_v = lax.all_gather(values, 'pb', axis=1, tiled=True)  14.9 us
    all_gather x1, blocking collectives, body(): piece_dk = lax.all_gather(tangent_k, 'pb', axis=1, tiled=True)  14 us
    add x7, other arithmetic, join_partials(): tnumer = first[3] * left[..., None] + second[3] * right[..., None]  11.9 us
    all_gather x1, blocking collectives, body(): lax.all_gather(tangent_q, 'ka', axis=1, tiled=True)  10.8 us
  transfers between devices with their start and end apart: 2, of which 2 were waited for; matrix products, arithmetic and copies ran while one was open for 2% of the time, Pallas kernels for 0%

commit v1 on v0

--- a/solution.py
+++ b/solution.py
@@ -45,7 +45,12 @@
     )
     piece_k = lax.all_gather(keys, "pb", axis=1, tiled=True)
     piece_dk = lax.all_gather(tangent_k, "pb", axis=1, tiled=True)
-    piece_v = lax.all_gather(values, "pb", axis=1, tiled=True)
+    ring = [values]
+    for hop in range(3):
+        ring.append(lax.ppermute(ring[-1], "pb", [(dev, (dev + 1) % 4) for dev in range(4)]))
+    piece_v = jnp.roll(
+        jnp.concatenate(ring[::-1], axis=1), (lax.axis_index("pb") + 1) * ring[0].shape[1], axis=1
+    )
     piece_dv = lax.all_gather(tangent_v, "pb", axis=1, tiled=True)
     shaped = (
         start_state[0].reshape(head_count, blocks, block),

time: 215 us -> 204 us (0.949)
  blocking collectives: 109 us -> 92.2 us
  starting transfers between devices: 0.08 us -> 4.44 us
    all_gather x1 -> x0, blocking collectives: 14.9 us -> none  [body(): piece_v = lax.all_gather(values, 'pb', axis=1, tiled=True)]
    ppermute x0 -> x3, starting transfers between devices: none -> 4.37 us  [body(): lax.ppermute(ring[-1], 'pb', [(dev, (dev + 1) % 4) for dev in range(4)])]
  transfers between devices with their start and end apart: 2 -> 5, of which waited for: 2 -> 2; matrix products, arithmetic and copies ran while one was open for 2% -> 3% of each run, Pallas kernels for 0% -> 0%
where the time goes in v1:
time: 204 us; the launch traced here: 203 us
  blocking collectives  92.2 us (45%)
  waiting for transfers between devices  42.4 us (21%)
  matrix products  23.9 us (12%)
  between operations  14.2 us (7%)
  other arithmetic  13.6 us (7%)
  local copies, waits for them, and re-layouts  12.4 us (6%)
  starting transfers between devices  4.44 us (2%)
    all_gather x2, waiting for transfers between devices, combined_all(): pieces = jax.tree.map(lambda part: lax.all_gather(part, axis), value)  41.7 us
    all_gather x3, blocking collectives, combined_all(): pieces = jax.tree.map(lambda part: lax.all_gather(part, axis), value)  26.4 us
    all_gather x1, blocking collectives, body(): piece_dv = lax.all_gather(tangent_v, 'pb', axis=1, tiled=True)  15.8 us
    all_gather x1, blocking collectives, body(): piece_dk = lax.all_gather(tangent_k, 'pb', axis=1, tiled=True)  14.9 us
    all_gather x1, blocking collectives, body(): piece_k = lax.all_gather(keys, 'pb', axis=1, tiled=True)  14.3 us
    add x7, other arithmetic, join_partials(): tnumer = first[3] * left[..., None] + second[3] * right[..., None]  11.9 us
    all_gather x1, blocking collectives, body(): lax.all_gather(tangent_q, 'ka', axis=1, tiled=True)  10.8 us
    all_gather x1, blocking collectives, body(): lax.all_gather(queries, 'ka', axis=1, tiled=True)  10.1 us
  transfers between devices with their start and end apart: 5, of which 2 were waited for; matrix products, arithmetic and copies ran while one was open for 3% of the time, Pallas kernels for 0%

profile of v1, /device:TPU:0, one launch (start us, length us, event | category | flops | bytes accessed | tf_op | source)
XLA Modules:
  0.0 203.3 jit_solution(11453829202141541786)
XLA Ops:
  7.2 3.1 %collective-permute-start = (f32[1,128,128]{2,1,0:T(8,128)}, f32[1,128,128]{2,1,0:T(8,128)S(1)}, u32[]{:S(2)}, u32[]{:S(2)}) collective-permute-start(f32[1,128,128]{2,1,0:T(8,128)} %param.12), channel_id=1, source_target_pairs={{0,8},{8,16},{16,24},{24,0},{1,9},{9,17},{17,25},{25,1},{2,10},{10... | collective-permute-start | bytes 196616 | tf_op jit(solution)/shard_map/ppermute | solution.py:50
  10.3 10.1 %all_gather.30 = f32[1,1024,128]{2,1,0:T(8,128)S(1)} all-gather(f32[1,128,128]{2,1,0:T(8,128)} %param.10), channel_id=1, replica_groups=mesh['pb'=4,'ka'=8] {'ka'}, dimensions={1}, use_global_device_ids=true | all-gather | bytes 589824 | tf_op jit(solution)/shard_map/all_gather | solution.py:31
  20.5 10.8 %all_gather.33 = f32[1,1024,128]{2,1,0:T(8,128)} all-gather(f32[1,128,128]{2,1,0:T(8,128)} %param.13), channel_id=1, replica_groups=mesh['pb'=4,'ka'=8] {'ka'}, dimensions={1}, use_global_device_ids=true | all-gather | bytes 589824 | tf_op jit(solution)/shard_map/all_gather | solution.py:32
  31.2 14.3 %all_gather.31 = f32[1,512,128]{2,1,0:T(8,128)S(1)} all-gather(f32[1,128,128]{2,1,0:T(8,128)} %param.11), channel_id=1, replica_groups=mesh['pb'=4,'ka'=8] {'pb'}, dimensions={1}, use_global_device_ids=true | all-gather | bytes 327680 | tf_op jit(solution)/shard_map/all_gather | solution.py:46
  45.8 14.9 %all_gather.34 = f32[1,512,128]{2,1,0:T(8,128)S(1)} all-gather(f32[1,128,128]{2,1,0:T(8,128)} %param.14), channel_id=1, replica_groups=mesh['pb'=4,'ka'=8] {'pb'}, dimensions={1}, use_global_device_ids=true | all-gather | bytes 327680 | tf_op jit(solution)/shard_map/all_gather | solution.py:47
  61.6 15.8 %all_gather.32 = f32[1,512,128]{2,1,0:T(8,128)} all-gather(f32[1,128,128]{2,1,0:T(8,128)} %param.15), channel_id=1, replica_groups=mesh['pb'=4,'ka'=8] {'pb'}, dimensions={1}, use_global_device_ids=true | all-gather | bytes 327680 | tf_op jit(solution)/shard_map/all_gather | solution.py:54
  79.2 24.6 %while.53 = (s32[]{:T(128)}, f32[2,512]{1,0:T(2,128)S(1)}, f32[2,512]{1,0:T(2,128)S(1)}, f32[2,512,128]{2,1,0:T(8,128)}, f32[2,512,128]{2,1,0:T(8,128)}, /*index...) while((s32[]{:T(128)}, f32[2,512]{1,0:T(2,128)S(1)}, ...), condition=%wide.region_4.5_spmd, body=%wide.region_0.4_spmd.sunk | while | flops 2419001344 | bytes 12892333 | solution.py:99
  79.2 1.9 fusion.66
  83.7 2.8 %convolution_add_fusion.5 = f32[512,128]{1,0:T(8,128)S(1)} fusion(f32[512,128]{1,0:T(8,128)} %get-tuple-element.549, f32[512,512]{0,1:T(8,128)S(1)} %get-tuple-element.489, f32[512]{0:T(512)S(1)} %get-tuple-element.488, f32[512]{0:T(512)S(1)} %get-tuple-element.492), kind=kOutput, calls=%fused_computation.7.clone.1 | convolution fusion | flops 402980864 | bytes 1576960 | tf_op jit(solution)/shard_map/while/body/eval_jaxpr/while/body/eval_jaxpr/dot_general | solution.py:93
  86.5 2.5 %fusion.71 = f32[2,512,128]{2,1,0:T(8,128)} fusion(f32[2,512,128]{2,1,0:T(8,128)} %get-tuple-element.530, s32[]{:T(128)S(6)} %copy.26, f32[512,128]{1,0:T(8,128)S(1)} %convolution_add_fusion.5, f32[512,512]{0,1:T(8,128)S(1)} %get-tuple-element.493, f32[512,128]{1,0:T(8,128)S(1)} %get-tuple-element.548), kind=kOutput, calls=%fused_computation.6.clone.1 | convolution fusion | flops 402718720 | bytes 1835012 | tf_op jit(solution)/shard_map/while/body/eval_jaxpr/while/body/eval_jaxpr/dot_general | solution.py:94
  89.0 2.5 %fusion.70 = f32[2,512,128]{2,1,0:T(8,128)} fusion(f32[2,512,128]{2,1,0:T(8,128)} %get-tuple-element.529, s32[]{:T(128)S(6)} %copy.26, f32[512,128]{1,0:T(8,128)S(1)} %get-tuple-element.548, f32[512,512]{0,1:T(8,128)S(1)} %get-tuple-element.489, f32[512]{0:T(512)S(1)} %get-tuple-element.488, f32[512]{0:T(512)S(1)} %get-tuple-element.492), kind=kOutput, calls=%fused_computation.10.clone.1 | convolution fusion | flops 402980864 | bytes 1576964 | tf_op jit(solution)/shard_map/while/body/eval_jaxpr/while/body/eval_jaxpr/dot_general | solution.py:90
  91.5 1.9 fusion.66
  96.0 2.8 %convolution_add_fusion.5 = f32[512,128]{1,0:T(8,128)S(1)} fusion(f32[512,128]{1,0:T(8,128)} %get-tuple-element.549, f32[512,512]{0,1:T(8,128)S(1)} %get-tuple-element.489, f32[512]{0:T(512)S(1)} %get-tuple-element.488, f32[512]{0:T(512)S(1)} %get-tuple-element.492), kind=kOutput, calls=%fused_computation.7.clone.1 | convolution fusion | flops 402980864 | bytes 1576960 | tf_op jit(solution)/shard_map/while/body/eval_jaxpr/while/body/eval_jaxpr/dot_general | solution.py:93
  98.8 2.5 %fusion.71 = f32[2,512,128]{2,1,0:T(8,128)} fusion(f32[2,512,128]{2,1,0:T(8,128)} %get-tuple-element.530, s32[]{:T(128)S(6)} %copy.26, f32[512,128]{1,0:T(8,128)S(1)} %convolution_add_fusion.5, f32[512,512]{0,1:T(8,128)S(1)} %get-tuple-element.493, f32[512,128]{1,0:T(8,128)S(1)} %get-tuple-element.548), kind=kOutput, calls=%fused_computation.6.clone.1 | convolution fusion | flops 402718720 | bytes 1835012 | tf_op jit(solution)/shard_map/while/body/eval_jaxpr/while/body/eval_jaxpr/dot_general | solution.py:94
  101.3 2.5 %fusion.70 = f32[2,512,128]{2,1,0:T(8,128)} fusion(f32[2,512,128]{2,1,0:T(8,128)} %get-tuple-element.529, s32[]{:T(128)S(6)} %copy.26, f32[512,128]{1,0:T(8,128)S(1)} %get-tuple-element.548, f32[512,512]{0,1:T(8,128)S(1)} %get-tuple-element.489, f32[512]{0:T(512)S(1)} %get-tuple-element.488, f32[512]{0:T(512)S(1)} %get-tuple-element.492), kind=kOutput, calls=%fused_computation.10.clone.1 | convolution fusion | flops 402980864 | bytes 1576964 | tf_op jit(solution)/shard_map/while/body/eval_jaxpr/while/body/eval_jaxpr/dot_general | solution.py:90
  104.7 8.8 %all_gather.36 = f32[8,1,1024]{2,1,0:T(1,128)S(1)} all-gather(f32[1,1,1024]{2,1,0:T(1,128)S(1)} %all_gather_reshape.16), channel_id=1, replica_groups=mesh['pb'=4,'ka'=8] {'ka'}, dimensions={0}, use_global_device_ids=true | all-gather | bytes 36864 | tf_op jit(solution)/shard_map/all_gather | solution.py:8
  113.5 8.6 %all_gather.35 = f32[8,1,1024]{2,1,0:T(1,128)S(1)} all-gather(f32[1,1,1024]{2,1,0:T(1,128)S(1)} %all_gather_reshape.15), channel_id=1, replica_groups=mesh['pb'=4,'ka'=8] {'ka'}, dimensions={0}, use_global_device_ids=true | all-gather | bytes 36864 | tf_op jit(solution)/shard_map/all_gather | solution.py:8
  122.1 9.0 %all_gather.39 = f32[8,1,1024]{2,1,0:T(1,128)S(1)} all-gather(f32[1,1,1024]{2,1,0:T(1,128)S(1)} %all_gather_reshape.19), channel_id=1, replica_groups=mesh['pb'=4,'ka'=8] {'ka'}, dimensions={0}, use_global_device_ids=true | all-gather | bytes 36864 | tf_op jit(solution)/shard_map/all_gather | solution.py:8
  131.1 8.4 %all-gather.5.cloned.1.call-done = f32[8,1,1024,128]{3,2,1,0:T(8,128)} async-done(((f32[1,1,1024,128]{3,2,1,0:T(8,128)}), f32[8,1,1024,128]{3,2,1,0:T(8,128)}) %all-gather.5.cloned.1.call-update) | async-done | bytes 4194320 | tf_op jit(solution)/shard_map/all_gather | solution.py:8
  139.5 4.1 %slice.48 = f32[7,1,1024,128]{3,2,1,0:T(8,128)} slice(f32[8,1,1024,128]{3,2,1,0:T(8,128)} %all-gather.5.cloned.1.call-done), slice={[1:8], [0:1], [0:1024], [0:128]} | slice | bytes 7340032 | tf_op jit(solution)/shard_map/slice | solution.py:10
  144.7 33.3 %all-gather.3.cloned.1.call-done = f32[8,1,1024,128]{3,2,1,0:T(8,128)} async-done(((f32[1,1,1024,128]{3,2,1,0:T(8,128)}), f32[8,1,1024,128]{3,2,1,0:T(8,128)}) %all-gather.3.cloned.1.call-update) | async-done | bytes 4194320 | tf_op jit(solution)/shard_map/all_gather | solution.py:8
  179.1 4.1 %slice.47 = f32[7,1,1024,128]{3,2,1,0:T(8,128)} slice(f32[8,1,1024,128]{3,2,1,0:T(8,128)} %all-gather.3.cloned.1.call-done), slice={[1:8], [0:1], [0:1024], [0:128]} | slice | bytes 7340032 | tf_op jit(solution)/shard_map/slice | solution.py:10
  183.2 12.5 %while.54 = (s32[]{:T(128)}, f32[1,1024]{1,0:T(1,128)S(1)}, f32[1,1024]{1,0:T(1,128)S(1)}, f32[1,1024,128]{2,1,0:T(8,128)S(1)}, f32[1,1024,128]{2,1,0:T(8,128)S(...) while((s32[]{:T(128)}, f32[1,1024]{1,0:T(1,128)S(1)}, ...), condition=%wide.region_6.7_spmd, body=%wide.region_5.6_spmd.sunk | while | flops 795650 | bytes 3207305 | solution.py:11
  183.2 1.7 fusion.74
  (81 shorter events, 22.5 us)
Async XLA Ops:
  7.2 132.4 %all-gather.5.cloned.1.call-start = ((), (), s32[]{:S(2)}) async-start(), calls=%async_computation.1 | async-start | bytes 4718592 | tf_op jit(solution)/shard_map/all_gather | solution.py:8
  7.2 38.3 %collective-permute-start = (f32[1,128,128]{2,1,0:T(8,128)}, f32[1,128,128]{2,1,0:T(8,128)S(1)}, u32[]{:S(2)}, u32[]{:S(2)}) collective-permute-start(f32[1,128,128]{2,1,0:T(8,128)} %param.12), channel_id=1, source_target_pairs={{0,8},{8,16},{16,24},{24,0},{1,9},{9,17},{17,25},{25,1},{2,10},{10... | collective-permute-start | bytes 196616 | tf_op jit(solution)/shard_map/ppermute | solution.py:50
  45.5 15.1 %collective-permute-start.1 = (f32[1,128,128]{2,1,0:T(8,128)S(1)}, f32[1,128,128]{2,1,0:T(8,128)S(1)}, u32[]{:S(2)}, u32[]{:S(2)}) collective-permute-start(f32[1,128,128]{2,1,0:T(8,128)S(1)} %collective-permute-done), channel_id=1, source_target_pairs={{0,8},{8,16},{16,24},{24,0},{1,9},{9,17},{17,25},{25,1},{2,10},{10... | collective-permute-start | bytes 196616 | tf_op jit(solution)/shard_map/ppermute | solution.py:50
  60.6 16.8 %collective-permute-start.2 = (f32[1,128,128]{2,1,0:T(8,128)S(1)}, f32[1,128,128]{2,1,0:T(8,128)S(1)}, u32[]{:S(2)}, u32[]{:S(2)}) collective-permute-start(f32[1,128,128]{2,1,0:T(8,128)S(1)} %collective-permute-done.1), channel_id=1, source_target_pairs={{0,8},{8,16},{16,24},{24,0},{1,9},{9,17},{17,25},{25,1},{2,10},{10... | collective-permute-start | bytes 196616 | tf_op jit(solution)/shard_map/ppermute | solution.py:50
  103.9 74.1 %all-gather.3.cloned.1.call-start = ((), (), s32[]{:S(2)}) async-start(), calls=%async_computation | async-start | bytes 4718592 | tf_op jit(solution)/shard_map/all_gather | solution.py:8
  113.5 31.2 %copy-start = (f32[8,1,1024]{2,1,0:T(1,128)}, f32[8,1,1024]{2,1,0:T(1,128)S(1)}, u32[]{:S(2)}) copy-start(f32[8,1,1024]{2,1,0:T(1,128)S(1)} %all_gather.36) | copy-start | bytes 98308
  122.1 22.6 %copy-start.1 = (f32[8,1,1024]{2,1,0:T(1,128)}, f32[8,1,1024]{2,1,0:T(1,128)S(1)}, u32[]{:S(2)}) copy-start(f32[8,1,1024]{2,1,0:T(1,128)S(1)} %all_gather.35) | copy-start | bytes 98308
  131.1 13.6 %copy-start.2 = (f32[8,1,1024]{2,1,0:T(1,128)}, f32[8,1,1024]{2,1,0:T(1,128)S(1)}, u32[]{:S(2)}) copy-start(f32[8,1,1024]{2,1,0:T(1,128)S(1)} %all_gather.39) | copy-start | bytes 98308
  178.0 5.2 %slice-start = ((f32[8,1,1024]{2,1,0:T(1,128)}), f32[7,1,1024]{2,1,0:T(1,128)S(1)}, s32[]{:S(2)}) async-start(f32[8,1,1024]{2,1,0:T(1,128)} %copy-done), calls=%async_computation.2 | async-start | bytes 57344 | tf_op jit(solution)/shard_map/slice | solution.py:10
  178.0 5.2 %slice-start.1 = ((f32[8,1,1024]{2,1,0:T(1,128)}), f32[7,1,1024]{2,1,0:T(1,128)S(1)}, s32[]{:S(2)}) async-start(f32[8,1,1024]{2,1,0:T(1,128)} %copy-done.1), calls=%async_computation.3 | async-start | bytes 57344 | tf_op jit(solution)/shard_map/slice | solution.py:10
  178.0 5.2 %slice-start.2 = ((f32[8,1,1024]{2,1,0:T(1,128)}), f32[7,1,1024]{2,1,0:T(1,128)S(1)}, s32[]{:S(2)}) async-start(f32[8,1,1024]{2,1,0:T(1,128)} %copy-done.2), calls=%async_computation.4 | async-start | bytes 57344 | tf_op jit(solution)/shard_map/slice | solution.py:10
Sparse Core Ops, SparseCore 0:
  104.0 35.4 all-gather.4
  141.4 36.5 all-gather.2
